TPU v7x, 32 devices: a whole 2x2x4 slice. The times are simulated.
32 devices in a mesh: dp: 8 (over z, y), mp: 4 (over x, core).
Axes of the slice: x: 2, y: 2, z: 4, core: 2. Of those that a mesh axis runs over, the one named last changes fastest.
Arguments:
- frames: int32 [48], P('dp'), may hold values from 17 to 129, as said below
- owners: int32 [240], P('dp'), may hold values from -1 to 7, as said below
- offsets: int32 [240], P('dp'), may hold values from -1 to 17, as said below
- groups: int32 [48], P('dp'), may hold values from 0 to 3, as said below
- latent: bfloat16 [240, 64, 128], P('dp'), may hold values from -12 to 12
- noise_blocks: bfloat16 [240, 64, 128], P('dp'), may hold values from -6 to 6
- rewards: float32 [48], P('dp'), may hold values from -6 to 6
- embed_weight: bfloat16 [64, 3072], replicated, may hold values from -2 to 2
- norm_gain: float32 [3072], replicated, may hold values from 0 to 2
- mid_weight: bfloat16 [3072, 3072], P(None, 'mp'), may hold values from -1 to 1
- head_weight: bfloat16 [3072, 64], P('mp'), may hold values from -1 to 1
Outputs:
- prediction: bfloat16 [144, 64, 128], P('dp')
- log_prob: float32 [48], P('dp')
- advantage: float32 [48], P('dp')
Inputs may be any that keep to these rules, and one draw needn't show every extreme that they name: frames = 4 m + 1 for a whole m; the block counts (frames - 1) // 32 + 1 of all samples add up to exactly 144, and some rollout device has all its samples at 129 frames. `owners`: a live slot names its owner, an empty one -1; every owner receives exactly 18 blocks; one rollout device sends at most 4 blocks to one owner, and in every draw some device sends that many to some owner. `offsets`: a live slot's row at its owner, rows distinct at each owner; empty slots -1. `groups`: every prompt has exactly 12 samples.
All inputs are finite; a program needn't handle non-finite values.
Results may differ from a plain program's by a relative error of at most 0.0068.
Values may be sent and summed in bfloat16 or wider, within the bound.
A program may use at most 64 MiB of HBM per device.

v0:
```python
import jax
import jax.numpy as jnp
from jax import lax
from jax.sharding import PartitionSpec as P

MAXB = 5
GSIZE = 12


def forward_blocks(pieces, embed_weight, norm_gain, mid_weight, head_weight):
    latent_part, noise_part = pieces
    embedded = jnp.einsum(
        "nct,cd->ntd", latent_part, embed_weight, preferred_element_type=jnp.float32
    )
    mean_sq = jnp.mean(embedded * embedded, axis=-1, keepdims=True)
    normed = (embedded * lax.rsqrt(mean_sq + 0.25) * norm_gain).astype(jnp.bfloat16)
    mid_out = jnp.einsum("ntd,df->ntf", normed, mid_weight, preferred_element_type=jnp.float32)
    activated = jax.nn.silu(mid_out).astype(jnp.bfloat16)
    partial_head = jnp.einsum(
        "ntf,fc->nct", activated, head_weight, preferred_element_type=jnp.float32
    )
    share = partial_head.shape[1] // lax.axis_size("mp")
    velocity_part = lax.psum_scatter(partial_head, "mp", scatter_dimension=1, tiled=True)
    noise_own = lax.dynamic_slice_in_dim(noise_part, lax.axis_index("mp") * share, share, 1)
    errors = noise_own.astype(jnp.float32) + velocity_part
    predicted = lax.all_gather(velocity_part.astype(jnp.bfloat16), "mp", axis=1, tiled=True)
    return (predicted, jnp.sum(errors * errors, axis=(1, 2)))


def local(
    frames,
    owners,
    offsets,
    groups,
    latent,
    noise_blocks,
    rewards,
    embed_weight,
    norm_gain,
    mid_weight,
    head_weight,
):
    per_device = frames.shape[0]
    devices = lax.axis_size("dp")
    slot_count = owners.shape[0]
    pair_cap = (slot_count + devices - 1) // devices
    owner_cap = 3 * per_device
    channels = latent.shape[1]
    block_len = latent.shape[2]
    samples = per_device * devices
    counts = (frames - 1) // 32 + 1
    slot_index = jnp.arange(slot_count, dtype=jnp.int32)
    live_slot = slot_index % MAXB < jnp.repeat(counts, MAXB)
    earlier = (
        (owners[:, None] == owners[None, :])
        & live_slot[None, :]
        & (slot_index[None, :] < slot_index[:, None])
    )
    places = jnp.sum(earlier.astype(jnp.int32), axis=1)
    target = jnp.where(live_slot, owners * pair_cap + places, devices * pair_cap)
    sample_ids = lax.axis_index("dp") * per_device + slot_index // MAXB
    meta = jnp.stack(
        [jnp.where(live_slot, offsets, -1), jnp.where(live_slot, sample_ids, -1)], axis=1
    )
    send_meta = jnp.full((devices * pair_cap, 2), -1, jnp.int32).at[target].set(meta, mode="drop")
    send_latent = (
        jnp.zeros((devices * pair_cap, channels, block_len), jnp.bfloat16)
        .at[target]
        .set(latent, mode="drop")
    )
    send_noise = (
        jnp.zeros((devices * pair_cap, channels, block_len), jnp.bfloat16)
        .at[target]
        .set(noise_blocks, mode="drop")
    )
    recv_latent, recv_noise, recv_meta = (
        lax.all_to_all(send_latent, "dp", split_axis=0, concat_axis=0, tiled=True),
        lax.all_to_all(send_noise, "dp", split_axis=0, concat_axis=0, tiled=True),
        lax.all_to_all(send_meta, "dp", split_axis=0, concat_axis=0, tiled=True),
    )
    dest_row = jnp.where(recv_meta[:, 0] >= 0, recv_meta[:, 0], owner_cap).astype(jnp.int32)
    owner_latent = (
        jnp.zeros((owner_cap, channels, block_len), jnp.bfloat16)
        .at[dest_row]
        .set(recv_latent, mode="drop")
    )
    owner_noise = (
        jnp.zeros((owner_cap, channels, block_len), jnp.bfloat16)
        .at[dest_row]
        .set(recv_noise, mode="drop")
    )
    owner_sample = (
        jnp.full((owner_cap,), -1, jnp.int32).at[dest_row].set(recv_meta[:, 1], mode="drop")
    )

    def run_group(pieces):
        return forward_blocks(pieces, embed_weight, norm_gain, mid_weight, head_weight)

    grouped = (
        owner_latent.reshape(3, per_device, channels, block_len),
        owner_noise.reshape(3, per_device, channels, block_len),
    )
    preds, slot_sums = lax.map(run_group, grouped)
    prediction = preds.reshape(owner_cap, channels, block_len)
    slot_sums = slot_sums.reshape(owner_cap)
    slot_sums = lax.psum(slot_sums, "mp")
    all_samples = jnp.arange(samples, dtype=jnp.int32)
    per_sample = jnp.sum(
        jnp.where(owner_sample[:, None] == all_samples[None, :], slot_sums[:, None], 0.0), axis=0
    )
    group_count = samples // GSIZE
    in_group = groups[:, None] == jnp.arange(group_count, dtype=jnp.int32)[None, :]
    group_sum = jnp.sum(jnp.where(in_group, rewards[:, None], 0.0), axis=0)
    group_sq = jnp.sum(jnp.where(in_group, (rewards * rewards)[:, None], 0.0), axis=0)
    own_sums = lax.psum_scatter(per_sample, "dp", scatter_dimension=0, tiled=True)
    group_sum, group_sq = lax.psum((group_sum, group_sq), "dp")
    log_prob = -0.5 * own_sums / (counts * block_len * channels).astype(jnp.float32)
    group_mean = group_sum / GSIZE
    variance = group_sq / GSIZE - group_mean * group_mean
    spread = jnp.sqrt(variance + 0.25)
    own_mean = jnp.sum(jnp.where(in_group, group_mean[None, :], 0.0), axis=1)
    own_spread = jnp.sum(jnp.where(in_group, spread[None, :], 0.0), axis=1)
    advantage = (rewards - own_mean) / own_spread
    return (prediction, log_prob, advantage)


def solution(mesh):
    placed = (
        P("dp"),
        P("dp"),
        P("dp"),
        P("dp"),
        P("dp", None, None),
        P("dp", None, None),
        P("dp"),
        P(),
        P(),
        P(None, "mp"),
        P("mp", None),
    )
    return jax.shard_map(
        local,
        mesh=mesh,
        in_specs=placed,
        out_specs=(P("dp", None, None), P("dp"), P("dp")),
        check_vma=False,
    )
```

profile of v0, /device:TPU:0, one launch (start us, length us, event | category | flops | bytes accessed | tf_op | source)
XLA Modules:
  0.0 223.9 jit_solution(7510934295319873025)
XLA Ops:
  8.8 0.9 convert_reduce_fusion
  11.2 0.7 copy.22
  11.9 7.3 %all-to-all-start = ((s32[8,4,2]{1,2,0:T(2,128)}), s32[8,4,2]{1,2,0:T(2,128)S(1)}, u32[]{:S(2)}, u32[]{:S(2)}) async-start(s32[8,4,2]{1,2,0:T(2,128)} %copy.22), calls=%async_computation.1 | async-start | bytes 16384 | tf_op jit(solution)/shard_map/all_to_all | solution.py:79
  19.2 0.9 broadcast.192.clone
  20.1 4.8 %scatter_fusion = bf16[32,64,128]{2,1,0:T(8,128)(2,1)} fusion(bf16[32,64,128]{2,1,0:T(8,128)(2,1)} %broadcast.192.clone, s32[30]{0:T(128)S(1)} %compare_select_fusion.2, bf16[30,64,128]{2,1,0:T(8,128)(2,1)} %param.17), kind=kCustom, calls=%fused_computation.1 | custom fusion | bytes 1474680 | tf_op jit(solution)/shard_map/scatter | solution.py:69
  24.9 0.8 all-to-all-done
  25.7 5.4 %all-to-all-start.1 = ((bf16[32,64,128]{2,1,0:T(8,128)(2,1)}), bf16[32,64,128]{2,1,0:T(8,128)(2,1)S(1)}, u32[]{:S(2)}, u32[]{:S(2)}) async-start(bf16[32,64,128]{2,1,0:T(8,128)(2,1)} %scatter_fusion), calls=%async_computation.2 | async-start | bytes 1048576 | tf_op jit(solution)/shard_map/all_to_all | solution.py:77
  31.1 0.9 broadcast.192.clone.1
  32.1 4.8 %scatter_fusion.2 = bf16[32,64,128]{2,1,0:T(8,128)(2,1)} fusion(bf16[32,64,128]{2,1,0:T(8,128)(2,1)} %broadcast.192.clone.1, s32[30]{0:T(128)S(1)} %compare_select_fusion.2, bf16[30,64,128]{2,1,0:T(8,128)(2,1)} %param.18), kind=kCustom, calls=%fused_computation.3 | custom fusion | bytes 1474680 | tf_op jit(solution)/shard_map/scatter | solution.py:74
  36.8 8.3 %all-to-all-done.1 = bf16[32,64,128]{2,1,0:T(8,128)(2,1)S(1)} async-done(((bf16[32,64,128]{2,1,0:T(8,128)(2,1)}), bf16[32,64,128]{2,1,0:T(8,128)(2,1)S(1)}, u32[]{:S(2)}, u32[]{:S(2)}) %all-to-all-start.1) | async-done | bytes 524320 | tf_op jit(solution)/shard_map/all_to_all | solution.py:77
  45.1 3.6 %all-to-all-start.2 = ((bf16[32,64,128]{2,1,0:T(8,128)(2,1)}), bf16[32,64,128]{2,1,0:T(8,128)(2,1)S(1)}, u32[]{:S(2)}, u32[]{:S(2)}) async-start(bf16[32,64,128]{2,1,0:T(8,128)(2,1)} %scatter_fusion.2), calls=%async_computation.3 | async-start | bytes 1048576 | tf_op jit(solution)/shard_map/all_to_all | solution.py:78
  51.0 1.6 scatter_fusion.1
  52.7 10.3 %all-to-all-done.2 = bf16[32,64,128]{2,1,0:T(8,128)(2,1)S(1)} async-done(((bf16[32,64,128]{2,1,0:T(8,128)(2,1)}), bf16[32,64,128]{2,1,0:T(8,128)(2,1)S(1)}, u32[]{:S(2)}, u32[]{:S(2)}) %all-to-all-start.2) | async-done | bytes 524320 | tf_op jit(solution)/shard_map/all_to_all | solution.py:78
  63.1 1.6 scatter_fusion.3
  64.7 124.3 %while.15 = (s32[]{:T(128)}, bf16[3,6,64,128]{3,2,1,0:T(8,128)(2,1)S(1)}, f32[3,6]{1,0:T(4,128)S(1)}, bf16[3,6,64,128]{3,2,1,0:T(8,128)(2,1)S(1)}, bf16[64,3072]...) while((s32[]{:T(128)}, ...), condition=%wide.region_10.11_spmd, body=%wide.region_6.10_spmd.sunk | while | flops 4016173824 | bytes 25559424 | solution.py:103
  64.8 5.0 %multiply_reduce_fusion.2 = (f32[6,128]{1,0:T(8,128)S(1)}, f32[6,128,3072]{2,1,0:T(8,128)}) fusion(bf16[64,3072]{1,0:T(8,128)(2,1)S(1)} %get-tuple-element.279, bf16[3,6,64,128]{3,2,1,0:T(8,128)(2,1)S(1)} %get-tuple-element.278, s32[]{:T(128)S(6)} %copy.35), kind=kOutput, calls=%fused_computation.7.clone.1 | convolution fusion | flops 306707712 | bytes 9931780 | tf_op jit(solution)/shard_map/while/body/eval_jaxpr/nct,cd->ntd/dot_general | solution.py:12
  69.8 10.3 %fusion.39 = f32[6,64,128]{2,1,0:T(8,128)} fusion(bf16[3072,768]{1,0:T(8,128)(2,1)} %get-tuple-element.281, f32[6,128,3072]{2,1,0:T(8,128)} %get-tuple-element.239, f32[3072]{0:T(1024)S(1)} %get-tuple-element.280, f32[6,128]{1,0:T(8,128)S(1)} %add_rsqrt_fusion.2, bf16[768,64]{0,1:T(8,128)(2,1)S(1)} %get-tuple-element.282), kind=kOutput, calls=%fused_computation.15.clone.1 | convolution fusion | flops 3709403136 | bytes 14466048 | tf_op jit(solution)/shard_map/while/body/eval_jaxpr/ntf,fc->nct/dot_general | solution.py:19
  80.2 18.9 %reduce-scatter.2.cloned.1.call-done = f32[6,16,128]{2,1,0:T(8,128)} async-done(((f32[6,64,128]{2,1,0:T(8,128)}), f32[6,16,128]{2,1,0:T(8,128)}) %reduce-scatter.2.cloned.1.call-update) | async-done | bytes 49168 | tf_op jit(solution)/shard_map/while/body/eval_jaxpr/reduce_scatter | solution.py:23
  99.1 1.0 fusion.40
  100.1 5.3 %all_gather.8 = bf16[6,64,128]{2,1,0:T(8,128)(2,1)S(1)} all-gather(bf16[6,16,128]{2,1,0:T(8,128)(2,1)S(1)} %get-tuple-element.241), channel_id=1, replica_groups=mesh['dp'=8,'mp'=4] {'mp'}, dimensions={1}, use_global_device_ids=true | all-gather | bytes 122880 | tf_op jit(solution)/shard_map/while/body/eval_jaxpr/all_gather | solution.py:26
  105.6 5.0 %multiply_reduce_fusion.2 = (f32[6,128]{1,0:T(8,128)S(1)}, f32[6,128,3072]{2,1,0:T(8,128)}) fusion(bf16[64,3072]{1,0:T(8,128)(2,1)S(1)} %get-tuple-element.279, bf16[3,6,64,128]{3,2,1,0:T(8,128)(2,1)S(1)} %get-tuple-element.278, s32[]{:T(128)S(6)} %copy.35), kind=kOutput, calls=%fused_computation.7.clone.1 | convolution fusion | flops 306707712 | bytes 9931780 | tf_op jit(solution)/shard_map/while/body/eval_jaxpr/nct,cd->ntd/dot_general | solution.py:12
  110.6 10.3 %fusion.39 = f32[6,64,128]{2,1,0:T(8,128)} fusion(bf16[3072,768]{1,0:T(8,128)(2,1)} %get-tuple-element.281, f32[6,128,3072]{2,1,0:T(8,128)} %get-tuple-element.239, f32[3072]{0:T(1024)S(1)} %get-tuple-element.280, f32[6,128]{1,0:T(8,128)S(1)} %add_rsqrt_fusion.2, bf16[768,64]{0,1:T(8,128)(2,1)S(1)} %get-tuple-element.282), kind=kOutput, calls=%fused_computation.15.clone.1 | convolution fusion | flops 3709403136 | bytes 14466048 | tf_op jit(solution)/shard_map/while/body/eval_jaxpr/ntf,fc->nct/dot_general | solution.py:19
  120.9 20.0 %reduce-scatter.2.cloned.1.call-done = f32[6,16,128]{2,1,0:T(8,128)} async-done(((f32[6,64,128]{2,1,0:T(8,128)}), f32[6,16,128]{2,1,0:T(8,128)}) %reduce-scatter.2.cloned.1.call-update) | async-done | bytes 49168 | tf_op jit(solution)/shard_map/while/body/eval_jaxpr/reduce_scatter | solution.py:23
  140.9 1.0 fusion.40
  141.9 5.3 %all_gather.8 = bf16[6,64,128]{2,1,0:T(8,128)(2,1)S(1)} all-gather(bf16[6,16,128]{2,1,0:T(8,128)(2,1)S(1)} %get-tuple-element.241), channel_id=1, replica_groups=mesh['dp'=8,'mp'=4] {'mp'}, dimensions={1}, use_global_device_ids=true | all-gather | bytes 122880 | tf_op jit(solution)/shard_map/while/body/eval_jaxpr/all_gather | solution.py:26
  147.3 5.0 %multiply_reduce_fusion.2 = (f32[6,128]{1,0:T(8,128)S(1)}, f32[6,128,3072]{2,1,0:T(8,128)}) fusion(bf16[64,3072]{1,0:T(8,128)(2,1)S(1)} %get-tuple-element.279, bf16[3,6,64,128]{3,2,1,0:T(8,128)(2,1)S(1)} %get-tuple-element.278, s32[]{:T(128)S(6)} %copy.35), kind=kOutput, calls=%fused_computation.7.clone.1 | convolution fusion | flops 306707712 | bytes 9931780 | tf_op jit(solution)/shard_map/while/body/eval_jaxpr/nct,cd->ntd/dot_general | solution.py:12
  152.4 10.3 %fusion.39 = f32[6,64,128]{2,1,0:T(8,128)} fusion(bf16[3072,768]{1,0:T(8,128)(2,1)} %get-tuple-element.281, f32[6,128,3072]{2,1,0:T(8,128)} %get-tuple-element.239, f32[3072]{0:T(1024)S(1)} %get-tuple-element.280, f32[6,128]{1,0:T(8,128)S(1)} %add_rsqrt_fusion.2, bf16[768,64]{0,1:T(8,128)(2,1)S(1)} %get-tuple-element.282), kind=kOutput, calls=%fused_computation.15.clone.1 | convolution fusion | flops 3709403136 | bytes 14466048 | tf_op jit(solution)/shard_map/while/body/eval_jaxpr/ntf,fc->nct/dot_general | solution.py:19
  162.7 19.9 %reduce-scatter.2.cloned.1.call-done = f32[6,16,128]{2,1,0:T(8,128)} async-done(((f32[6,64,128]{2,1,0:T(8,128)}), f32[6,16,128]{2,1,0:T(8,128)}) %reduce-scatter.2.cloned.1.call-update) | async-done | bytes 49168 | tf_op jit(solution)/shard_map/while/body/eval_jaxpr/reduce_scatter | solution.py:23
  182.7 1.0 fusion.40
  183.7 5.3 %all_gather.8 = bf16[6,64,128]{2,1,0:T(8,128)(2,1)S(1)} all-gather(bf16[6,16,128]{2,1,0:T(8,128)(2,1)S(1)} %get-tuple-element.241), channel_id=1, replica_groups=mesh['dp'=8,'mp'=4] {'mp'}, dimensions={1}, use_global_device_ids=true | all-gather | bytes 122880 | tf_op jit(solution)/shard_map/while/body/eval_jaxpr/all_gather | solution.py:26
  189.1 6.0 %psum.21 = f32[18]{0:T(128)S(1)} all-reduce(f32[18]{0:T(128)S(1)} %reshape.132), channel_id=1, replica_groups=mesh['dp'=8,'mp'=4] {'mp'}, use_global_device_ids=true, to_apply=%region_12.13 | all-reduce | flops 18 | bytes 144 | tf_op jit(solution)/shard_map/psum | solution.py:106
  195.2 21.5 %all-reduce.1 = (f32[48]{0:T(128)S(1)}, f32[4]{0:T(128)S(1)}, f32[4]{0:T(128)S(1)}) all-reduce(f32[48]{0:T(128)S(1)} %select_reduce_fusion, f32[4]{0:T(128)S(1)} %get-tuple-element.145, f32[4]{0:T(128)S(1)} %get-tuple-element.146), channel_id=3, replica_groups=mesh['dp'=8,'mp'=4] {'dp'}, use_global_device_ids=true, to_apply=%region_14.15.clone | all-reduce | flops 56 | bytes 448
  (57 shorter events, 5.9 us)
Async XLA Ops:
  7.2 41.6 %copy-start.7 = (u32[32]{0:T(128)S(1)}, u32[32]{0:T(128)}, u32[]{:S(2)}) copy-start(u32[32]{0:T(128)} %constant.198) | copy-start | bytes 388
  7.2 41.6 %copy-start.2 = (f32[6]{0:T(128)S(1)}, f32[6]{0:T(128)}, u32[]{:S(2)}) copy-start(f32[6]{0:T(128)} %param.19) | copy-start | bytes 76
  7.2 42.8 %copy-start.1 = (s32[6]{0:T(128)S(1)}, s32[6]{0:T(128)}, u32[]{:S(2)}) copy-start(s32[6]{0:T(128)} %param.16) | copy-start | bytes 76
  11.9 13.8 %all-to-all-start = ((s32[8,4,2]{1,2,0:T(2,128)}), s32[8,4,2]{1,2,0:T(2,128)S(1)}, u32[]{:S(2)}, u32[]{:S(2)}) async-start(s32[8,4,2]{1,2,0:T(2,128)} %copy.22), calls=%async_computation.1 | async-start | bytes 16384 | tf_op jit(solution)/shard_map/all_to_all | solution.py:79
  20.1 44.6 %copy-start = (bf16[64,3072]{1,0:T(8,128)(2,1)S(1)}, bf16[64,3072]{1,0:T(8,128)(2,1)}, u32[]{:S(2)}) copy-start(bf16[64,3072]{1,0:T(8,128)(2,1)} %param.20) | copy-start | bytes 1179652
  20.1 44.6 %copy-start.5 = (bf16[768,64]{0,1:T(8,128)(2,1)S(1)}, bf16[768,64]{0,1:T(8,128)(2,1)}, u32[]{:S(2)}) copy-start(bf16[768,64]{0,1:T(8,128)(2,1)} %param.23) | copy-start | bytes 294916
  20.1 44.6 %copy-start.6 = (f32[3072]{0:T(1024)S(1)}, f32[3072]{0:T(1024)}, u32[]{:S(2)}) copy-start(f32[3072]{0:T(1024)} %param.21) | copy-start | bytes 36868
  25.7 19.4 %all-to-all-start.1 = ((bf16[32,64,128]{2,1,0:T(8,128)(2,1)}), bf16[32,64,128]{2,1,0:T(8,128)(2,1)S(1)}, u32[]{:S(2)}, u32[]{:S(2)}) async-start(bf16[32,64,128]{2,1,0:T(8,128)(2,1)} %scatter_fusion), calls=%async_computation.2 | async-start | bytes 1048576 | tf_op jit(solution)/shard_map/all_to_all | solution.py:77
  45.1 17.9 %all-to-all-start.2 = ((bf16[32,64,128]{2,1,0:T(8,128)(2,1)}), bf16[32,64,128]{2,1,0:T(8,128)(2,1)S(1)}, u32[]{:S(2)}, u32[]{:S(2)}) async-start(bf16[32,64,128]{2,1,0:T(8,128)(2,1)} %scatter_fusion.2), calls=%async_computation.3 | async-start | bytes 1048576 | tf_op jit(solution)/shard_map/all_to_all | solution.py:78
  64.7 152.1 %copy-start.3 = (s32[6]{0:T(128)S(1)}, s32[6]{0:T(128)}, u32[]{:S(2)}) copy-start(s32[6]{0:T(128)} %param.13) | copy-start | bytes 76
  64.7 34.4 %reduce-scatter.2.cloned.1.call-start = ((), (), s32[]{:S(2)}) async-start(), calls=%async_computation.4 | async-start | bytes 245760 | tf_op jit(solution)/shard_map/while/body/eval_jaxpr/reduce_scatter | solution.py:23
  105.5 35.4 %reduce-scatter.2.cloned.1.call-start = ((), (), s32[]{:S(2)}) async-start(), calls=%async_computation.4 | async-start | bytes 245760 | tf_op jit(solution)/shard_map/while/body/eval_jaxpr/reduce_scatter | solution.py:23
  147.3 35.4 %reduce-scatter.2.cloned.1.call-start = ((), (), s32[]{:S(2)}) async-start(), calls=%async_computation.4 | async-start | bytes 245760 | tf_op jit(solution)/shard_map/while/body/eval_jaxpr/reduce_scatter | solution.py:23
  189.0 28.4 %copy-start.4 = (bf16[3,6,64,128]{3,2,1,0:T(8,128)(2,1)}, bf16[3,6,64,128]{3,2,1,0:T(8,128)(2,1)S(1)}, u32[]{:S(2)}) copy-start(bf16[3,6,64,128]{3,2,1,0:T(8,128)(2,1)S(1)} %get-tuple-element.141) | copy-start | bytes 884740
Sparse Core Ops, SparseCore 0:
  80.3 18.7 reduce-scatter.1
  121.1 19.8 reduce-scatter.1
  162.8 19.7 reduce-scatter.1
where the time goes:
time: 224 us
  waiting for transfers between devices  78.3 us (35%)
  matrix products  46.1 us (21%)
  blocking collectives  43.4 us (19%)
  local copies, waits for them, and re-layouts  18.1 us (8%)
  starting transfers between devices  16.5 us (7%)
  between operations  14.5 us (6%)
  other arithmetic  6.95 us (3%)
    reduce_scatter x3, waiting for transfers between devices, forward_blocks(): lax.psum_scatter(partial_head, 'mp', scatter_dimension=1, tiled=True)  58.8 us
    dot_general x3, matrix products, forward_blocks(): jnp.einsum('ntf,fc->nct', activated, head_weight, preferred_element_type=...  30.9 us
    unnamed x1, blocking collectives  21.5 us
    all_gather x3, blocking collectives, forward_blocks(): lax.all_gather(velocity_part.astype(jnp.bfloat16), 'mp', axis=1, tiled=True)  15.9 us
    dot_general x3, matrix products, forward_blocks(): jnp.einsum('nct,cd->ntd', latent_part, embed_weight, preferred_element_ty...  15.1 us
    all_to_all x1, waiting for transfers between devices, local(): lax.all_to_all(send_noise, 'dp', split_axis=0, concat_axis=0, tiled=True)  10.3 us
    all_to_all x1, waiting for transfers between devices, local(): lax.all_to_all(send_latent, 'dp', split_axis=0, concat_axis=0, tiled=True)  8.26 us
    all_to_all x1, starting transfers between devices, local(): lax.all_to_all(send_meta, 'dp', split_axis=0, concat_axis=0, tiled=True)  7.31 us
  transfers between devices with their start and end apart: 6, of which 6 were waited for; matrix products, arithmetic and copies ran while one was open for 6% of the time, Pallas kernels for 0%

commit v1 on v0

v1 whole, which is shorter than its diff:
```python
import functools

import jax
import jax.numpy as jnp
from jax import lax
from jax.experimental import pallas as pl
from jax.experimental.pallas import tpu as pltpu
from jax.sharding import PartitionSpec as P

MAXB = 5
GSIZE = 12
F32 = jnp.float32
BF16 = jnp.bfloat16


def index_kernel(
    dims, frames, owners, offsets, groups, rewards, slots, info, count, row_of
):
    devices, cap, jm, bpc = dims
    for o in range(devices):
        count[o] = 0
    for i in range(devices * cap):
        slots[i] = -1
        row_of[i] = -1

    def place(i, z):
        live = i % MAXB < lax.shift_right_arithmetic(frames[i // MAXB] - 1, 5) + 1

        @pl.when(live)
        def _():
            o = owners[i]
            p = count[o]
            count[o] = p + 1
            slots[o * cap + p] = i
            row_of[o * cap + p] = offsets[i]

        return z

    lax.fori_loop(0, owners.shape[0], place, 0)
    row = lax.broadcasted_iota(jnp.int32, (8, 128), 0)
    lane = lax.broadcasted_iota(jnp.int32, (8, 128), 1)
    common = jnp.zeros((8, 128), F32)
    for i in range(frames.shape[0]):
        common = jnp.where((row == 1) & (lane == i), rewards[i], common)
        common = jnp.where((row == 2) & (lane == i), groups[i].astype(F32), common)

    def tile(o, z):
        t = common
        for j in range(cap):
            t = jnp.where((row == 0) & (lane == j), row_of[o * cap + j].astype(F32), t)
        info[o] = t
        return z

    lax.fori_loop(0, devices, tile, 0)


def main_kernel(
    dims, width, slots, embed, gain, head, info, latent, noise, mid,
    blocks, infos, errs,
    lat, noi, mids, tokens, wown, wbuf, wt, half, vel, pred, err, ebuf,
    wsend, wrecv, isend, irecv, psend, precv, gsend, grecv, esend, erecv, local_sem, load_sem,
):
    devices, cap, jm, bpc = dims
    c = embed.shape[0]
    bt = latent.shape[2]
    nchunk = tokens.shape[0]
    steps, kc, _ = mids.shape
    loads = [pltpu.make_async_copy(latent, lat, load_sem.at[0])]
    for i in range(steps):
        loads.append(
            pltpu.make_async_copy(mid.at[pl.ds(i * kc, kc)], mids.at[i], load_sem.at[1 + i])
        )
    loads.append(pltpu.make_async_copy(noise, noi, load_sem.at[1 + steps]))
    for cp in loads:
        cp.start()
    me = lax.axis_index("dp")
    m = lax.axis_index("mp")
    partner = m + 1 - 2 * (m % 2)
    across = (m + 2) % 4
    diag = (partner + 2) % 4

    def copy(src, dst, ssem, rsem, dp, mp):
        return pltpu.make_async_remote_copy(
            src_ref=src, dst_ref=dst, send_sem=ssem, recv_sem=rsem,
            device_id=(dp, mp), device_id_type=pl.DeviceIdType.MESH,
        )

    barrier = pltpu.get_barrier_semaphore()
    for p in (partner, across, diag):
        pl.semaphore_signal(
            barrier, inc=1, device_id=(me, p), device_id_type=pl.DeviceIdType.MESH
        )
    for d in range(1, devices):
        pl.semaphore_signal(
            barrier, inc=1, device_id=((me + d) % devices, m),
            device_id_type=pl.DeviceIdType.MESH,
        )
    w = embed[...]
    gram = lax.dot_general(w, w, (((1,), (1,)), ((), ())), preferred_element_type=F32)
    pl.semaphore_wait(barrier, 3 + devices - 1)

    def trio(src, part):
        return [
            copy(src, wbuf.at[0, part], wsend.at[0, part], wrecv.at[0, part], me, partner),
            copy(src, wbuf.at[1, part], wsend.at[1, part], wrecv.at[1, part], me, across),
            copy(
                wbuf.at[1, part], wbuf.at[2, part], wsend.at[2, part], wrecv.at[2, part],
                me, partner,
            ),
        ]

    hc = trio(head, 1)
    wc = trio(wown, 0)
    hc[1].start()
    hc[0].start()
    ic = [None]
    for d in range(1, devices):
        peer = (me + d) % devices
        cp = copy(info.at[peer], infos.at[me], isend.at[d], irecv.at[d], peer, m)
        cp.start()
        ic.append(cp)
    own_info = pltpu.make_async_copy(info.at[me], infos.at[me], local_sem.at[0])
    own_info.start()

    loads[0].wait()

    def prepare(k, z):
        for b in range(bpc):
            q = k * bpc + b
            s = jnp.maximum(slots[(q // jm) * cap + m * jm + q % jm], 0)
            tokens[k, :, b * bt : (b + 1) * bt] = lat[s]
        x = tokens[k].astype(F32)
        y = jnp.dot(gram, x, preferred_element_type=F32, precision=lax.Precision.HIGHEST)
        ms = jnp.maximum(jnp.sum(x * y, axis=0, keepdims=True), 0.0) / width
        half[k] = 0.5 * lax.rsqrt(ms + 0.25)
        return z

    lax.fori_loop(0, nchunk, prepare, 0)

    folded = None
    for i in range(steps):
        wg = embed[:, i * kc : (i + 1) * kc].astype(F32) * gain[:, i * kc : (i + 1) * kc]
        hi = wg.astype(BF16)
        lo = (wg - hi.astype(F32)).astype(BF16)
        loads[1 + i].wait()
        both = jnp.dot(
            jnp.concatenate([hi, lo], axis=0), mids[i], preferred_element_type=F32
        )
        folded = both if i == 0 else folded + both
    folded = folded[:c] + folded[c:]
    wown[...] = folded.astype(BF16)
    wt[...] = folded.T.astype(BF16)
    wc[1].start()
    wc[0].start()
    hc[1].wait_recv()
    hc[2].start()

    def part(href, k):
        u = jnp.dot(wt[...], tokens[k], preferred_element_type=F32)
        h = u * half[k]
        act = (h + h * jnp.tanh(h)).astype(BF16)
        return jnp.dot(href[...], act, preferred_element_type=F32)

    def share(href, first):
        def body(k, z):
            v = part(href, k)
            vel[k] = v if first else vel[k] + v
            return z

        lax.fori_loop(0, nchunk, body, 0)

    share(head, True)
    hc[0].wait_recv()
    wc[0].wait_recv()
    wt[...] = wbuf[0, 0].astype(F32).T.astype(BF16)
    share(wbuf.at[0, 1], False)
    wc[1].wait_recv()
    wc[2].start()
    wt[...] = wbuf[1, 0].astype(F32).T.astype(BF16)
    share(wbuf.at[1, 1], False)
    hc[2].wait_recv()
    wc[2].wait_recv()
    wt[...] = wbuf[2, 0].astype(F32).T.astype(BF16)
    err[...] = jnp.zeros_like(err)
    row = lax.broadcasted_iota(jnp.int32, err.shape, 0)
    loads[1 + steps].wait()

    def last(k, z):
        v = vel[k] + part(wbuf.at[2, 1], k)
        for b in range(bpc):
            q = k * bpc + b
            vb = v[:, b * bt : (b + 1) * bt]
            pred[q] = vb.astype(BF16)
            s = slots[(q // jm) * cap + m * jm + q % jm]
            e = noi[jnp.maximum(s, 0)].astype(F32) + vb
            e = jnp.sum(e * e, axis=0, keepdims=True)
            sample = jnp.where(s < 0, -1, s // MAXB)
            err[...] += jnp.where(row == sample, e, 0.0)
        return z

    lax.fori_loop(0, nchunk, last, 0)

    pc = [None]
    for d in range(1, devices):
        peer = (me + d) % devices
        cp = copy(
            pred.at[pl.ds(peer * jm, jm)], blocks.at[m, me], psend.at[d], precv.at[d], peer, m
        )
        cp.start()
        pc.append(cp)
    own = pltpu.make_async_copy(pred.at[pl.ds(me * jm, jm)], blocks.at[m, me], local_sem.at[1])
    own.start()
    ec = []
    for i, p in enumerate((partner, across, diag)):
        cp = copy(err, ebuf.at[i], esend.at[i], erecv.at[i], me, p)
        cp.start()
        ec.append(cp)

    gc = []
    for d in range(devices):
        src = (me - d + devices) % devices
        if d == 0:
            own.wait()
        else:
            pc[d].wait_recv()
        a = copy(
            blocks.at[m, src], blocks.at[m, src], gsend.at[0, d], grecv.at[0, d], me, across
        )
        b = copy(
            blocks.at[m, src], blocks.at[m, src], gsend.at[1, d], grecv.at[1, d], me, partner
        )
        a.start()
        b.start()
        gc += [a, b]
    relay = []
    for d in range(devices):
        src = (me - d + devices) % devices
        gc[2 * d].wait_recv()
        r = copy(
            blocks.at[across, src], blocks.at[across, src],
            gsend.at[2, d], grecv.at[2, d], me, partner,
        )
        r.start()
        relay.append(r)
    for i in range(3):
        ec[i].wait_recv()
    errs[...] = err[...] + ebuf[0] + ebuf[1] + ebuf[2]
    own_info.wait()
    for d in range(1, devices):
        ic[d].wait()
        pc[d].wait_send()
    for d in range(devices):
        gc[2 * d].wait_send()
        gc[2 * d + 1].wait()
        relay[d].wait()
    for i in range(3):
        hc[i].wait_send()
        wc[i].wait_send()
        ec[i].wait_send()


def place_kernel(rows, blocks, out):
    def body(k, z):
        r = rows[k]

        @pl.when(r >= 0)
        def _():
            out[r] = blocks[k]

        return z

    lax.fori_loop(0, blocks.shape[0], body, 0)


def local(
    frames, owners, offsets, groups, latent, noise_blocks, rewards,
    embed_weight, norm_gain, mid_weight, head_weight,
):
    spd = frames.shape[0]
    devices = lax.axis_size("dp")
    mp = lax.axis_size("mp")
    nslot, c, bt = latent.shape
    width = embed_weight.shape[1]
    hidden = mid_weight.shape[1]
    pair_cap = (nslot + devices - 1) // devices
    jm = (pair_cap + mp - 1) // mp
    cap = jm * mp
    bpc = 2 if devices * jm % 2 == 0 else 1
    nchunk = devices * jm // bpc
    dims = (devices, cap, jm, bpc)
    rows8 = (spd + 7) // 8 * 8
    steps = 4
    kc = width // steps
    smem = pl.BlockSpec(memory_space=pltpu.SMEM)
    vmem = pl.BlockSpec(memory_space=pltpu.VMEM)
    hbm = pl.BlockSpec(memory_space=pl.ANY)
    shape = jax.ShapeDtypeStruct
    slots, info = pl.pallas_call(
        functools.partial(index_kernel, dims),
        in_specs=[smem] * 5,
        out_specs=[smem, vmem],
        out_shape=[shape((devices * cap,), jnp.int32), shape((devices, 8, 128), F32)],
        scratch_shapes=[
            pltpu.SMEM((devices,), jnp.int32),
            pltpu.SMEM((devices * cap,), jnp.int32),
        ],
        name="index",
    )(frames, owners, offsets, groups, rewards)
    dma = pltpu.SemaphoreType.DMA
    blocks, infos, errs = pl.pallas_call(
        functools.partial(main_kernel, dims, width),
        in_specs=[smem] + [vmem] * 4 + [hbm] * 3,
        out_specs=[vmem] * 3,
        out_shape=[
            shape((mp, devices, jm, c, bt), BF16),
            shape((devices, 8, 128), F32),
            shape((rows8, bt), F32),
        ],
        scratch_shapes=[
            pltpu.VMEM((nslot, c, bt), BF16),
            pltpu.VMEM((nslot, c, bt), BF16),
            pltpu.VMEM((steps, kc, hidden), BF16),
            pltpu.VMEM((nchunk, c, bpc * bt), BF16),
            pltpu.VMEM((c, hidden), BF16),
            pltpu.VMEM((3, 2, c, hidden), BF16),
            pltpu.VMEM((hidden, c), BF16),
            pltpu.VMEM((nchunk, 1, bpc * bt), F32),
            pltpu.VMEM((nchunk, c, bpc * bt), F32),
            pltpu.VMEM((devices * jm, c, bt), BF16),
            pltpu.VMEM((rows8, bt), F32),
            pltpu.VMEM((3, rows8, bt), F32),
            dma((3, 2)), dma((3, 2)),
            dma((devices,)), dma((devices,)),
            dma((devices,)), dma((devices,)),
            dma((3, devices)), dma((3, devices)),
            dma((3,)), dma((3,)),
            dma((2,)), dma((steps + 2,)),
        ],
        compiler_params=pltpu.CompilerParams(collective_id=0, has_side_effects=True),
        name="exchange",
    )(
        slots, embed_weight, norm_gain.reshape(1, width), head_weight.T, info,
        latent, noise_blocks, mid_weight,
    )
    where = infos[:, 0, :cap].reshape(devices, mp, jm).transpose(1, 0, 2).reshape(-1)
    prediction = pl.pallas_call(
        place_kernel,
        in_specs=[smem, vmem],
        out_specs=vmem,
        out_shape=shape((3 * spd, c, bt), BF16),
        name="place",
    )(where.astype(jnp.int32), blocks.reshape(mp * devices * jm, c, bt))
    counts = (frames - 1) // 32 + 1
    log_prob = -0.5 * jnp.sum(errs[:spd], axis=1) / (counts * bt * c).astype(F32)
    all_rewards = infos[:, 1, :spd].reshape(-1)
    same = groups.astype(F32)[:, None] == infos[:, 2, :spd].reshape(-1)[None, :]
    mean = jnp.sum(jnp.where(same, all_rewards[None, :], 0.0), axis=1) / GSIZE
    meansq = jnp.sum(jnp.where(same, (all_rewards * all_rewards)[None, :], 0.0), axis=1) / GSIZE
    advantage = (rewards - mean) / jnp.sqrt(meansq - mean * mean + 0.25)
    return (prediction, log_prob, advantage)


def solution(mesh):
    placed = (
        P("dp"),
        P("dp"),
        P("dp"),
        P("dp"),
        P("dp", None, None),
        P("dp", None, None),
        P("dp"),
        P(),
        P(),
        P(None, "mp"),
        P("mp", None),
    )
    return jax.shard_map(
        local,
        mesh=mesh,
        in_specs=placed,
        out_specs=(P("dp", None, None), P("dp"), P("dp")),
        check_vma=False,
    )
```

time: 224 us -> 38.4 us (0.17)
  waiting for transfers between devices: 78.3 us -> 0 us
  matrix products: 46.1 us -> 0 us
  blocking collectives: 43.4 us -> 0 us
  Pallas kernels: 0 us -> 33.3 us
  starting transfers between devices: 16.5 us -> 0 us
  local copies, waits for them, and re-layouts: 18.1 us -> 1.79 us
  between operations: 14.5 us -> 0.69 us
  other arithmetic: 6.95 us -> 2.29 us
    reduce_scatter x3 -> x0, waiting for transfers between devices: 58.8 us -> none  [forward_blocks(): lax.psum_scatter(partial_head, 'mp', scatter_dimension=1, tiled=True)]
    dot_general x6 -> x0, matrix products: 46.1 us -> none  [the longest x3 30.9 us: forward_blocks(): jnp.einsum('ntf,fc->nct', activated, head_weight, preferred_element_type=...]
    pallas_call x0 -> x3, Pallas kernels: none -> 33.3 us  [the longest x1 28.6 us: local(): pl.pallas_call(functools.partial(main_kernel, dims, width), in_specs=[sme...]
    unnamed x1 -> x0, blocking collectives: 21.5 us -> none
    all_to_all x3 -> x0, waiting for transfers between devices: 19.4 us -> none  [the longest x1 10.3 us: local(): lax.all_to_all(send_noise, 'dp', split_axis=0, concat_axis=0, tiled=True)]
    all_to_all x3 -> x0, starting transfers between devices: 16.4 us -> none  [the longest x1 7.31 us: local(): lax.all_to_all(send_meta, 'dp', split_axis=0, concat_axis=0, tiled=True)]
    all_gather x3 -> x0, blocking collectives: 15.9 us -> none  [forward_blocks(): lax.all_gather(velocity_part.astype(jnp.bfloat16), 'mp', axis=1, tiled=True)]
    scatter x6 -> x0, local copies, waits for them, and re-layouts: 14.1 us -> none  [the longest x1 4.77 us: local(): send_noise = jnp.zeros((devices * pair_cap, channels, block_len), jnp.bfl...]
  transfers between devices with their start and end apart: 6 -> 0, of which waited for: 6 -> 0; matrix products, arithmetic and copies ran while one was open for 6% -> 0% of each run, Pallas kernels for 0% -> 0%
where the time goes in v1:
time: 38.4 us; the launch traced here: 38.1 us
  Pallas kernels  33.3 us (87%)
  other arithmetic  2.29 us (6%)
  local copies, waits for them, and re-layouts  1.79 us (5%)
  between operations  0.69 us (2%)
    pallas_call x1, Pallas kernels, local(): pl.pallas_call(functools.partial(main_kernel, dims, width), in_specs=[sme...  28.6 us
    pallas_call x1, Pallas kernels, local(): pl.pallas_call(functools.partial(index_kernel, dims), in_specs=[smem] * 5...  2.54 us
    pallas_call x1, Pallas kernels, local(): pl.pallas_call(place_kernel, in_specs=[smem, vmem], out_specs=vmem, out_s...  2.2 us
    slice x1, local copies, waits for them, and re-layouts, local(): same = groups.astype(F32)[:, None] == infos[:, 2, :spd].reshape(-1)[None, :]  0.86 us
    reduce_sum x1, other arithmetic, local(): jnp.sum(errs[:spd], axis=1)  0.8 us

profile of v1, /device:TPU:0, one launch (start us, length us, event | category | flops | bytes accessed | tf_op | source)
XLA Modules:
  0.0 38.1 jit_solution(7337872178253242713)
XLA Ops:
  0.6 0.0 copy-start
  0.6 0.0 copy-start.2
  0.7 0.0 copy-start.1
  0.7 2.5 %index.1 = (s32[32]{0:T(128)}, f32[8,8,128]{2,1,0:T(8,128)}) custom-call(s32[6]{0:T(128)} %frames.1, s32[30]{0:T(128)} %owners.1, s32[30]{0:T(128)} %offsets.1, s32[6]{0:T(128)} %groups.1, f32[6]{0:T(128)} %rewards.1), custom_call_target="tpu_custom_call" | custom-call | tf_op jit(solution)/shard_map/index/pallas_call | solution.py:298
  3.2 28.6 %exchange.1 = (bf16[4,8,1,64,128]{4,3,2,1,0:T(8,128)(2,1)}, f32[8,8,128]{2,1,0:T(8,128)}, f32[8,128]{1,0:T(8,128)}) custom-call(s32[32]{0:T(128)} %get-tuple-element.8.slots, bf16[64,3072]{1,0:T(8,128)(2,1)} %embed.1, f32[1,3072]{1,0:T(1,128)} %bitcast.10, bf16[64,768]{1,0:T(8,128)(2,1)} %bitcast.9, f32[8,8,128]{2,1,0:T(8,128)} %get-tuple-element.9.info, ...), custom_call_target="tpu_custom_call" | custom-call | tf_op jit(solution)/shard_map/exchange/pallas_call | solution.py:310
  31.8 0.9 %slice_reduce_fusion.1 = (f32[8,6]{1,0:T(8,128)S(1)}, f32[8,6]{1,0:T(8,128)S(1)}) fusion(f32[8,8,128]{2,1,0:T(8,128)} %get-tuple-element.10), kind=kLoop, calls=%fused_computation.5 | loop fusion | bytes 768 | tf_op jit(solution)/shard_map/slice | solution.py:356
  32.6 0.1 broadcast_in_dim.22
  32.7 0.1 eq.16
  32.8 0.0 copy-done.2
  32.8 0.2 fusion
  33.0 0.8 %slice_reduce_fusion.2 = f32[6]{0:T(128)S(1)} fusion(f32[8,128]{1,0:T(8,128)} %get-tuple-element.12), kind=kLoop, calls=%fused_computation.6 | loop fusion | flops 762 | bytes 3096 | tf_op jit(solution)/shard_map/reduce_sum | solution.py:354
  33.8 0.0 copy-done
  33.8 0.0 copy-done.1
  33.8 0.5 %rsqrt_multiply_fusion = (f32[6]{0:T(128)}, f32[6]{0:T(128)}) fusion(f32[6]{0:T(128)S(1)} %get-tuple-element.16, f32[6]{0:T(128)S(1)} %copy-done.1, f32[6]{0:T(128)S(1)} %get-tuple-element.15, s32[6]{0:T(128)S(1)} %copy-done, f32[6]{0:T(128)S(1)} %slice_reduce_fusion.2), kind=kLoop, calls=%fused_computation.12 | loop fusion | flops 168 | bytes 168 | tf_op jit(solution)/shard_map/div | solution.py:359
  34.4 0.8 %slice_convert_fusion = s32[8,1,4]{2,1,0:T(1,128)S(1)} fusion(f32[8,8,128]{2,1,0:T(8,128)} %get-tuple-element.10), kind=kLoop, calls=%fused_computation.7 | loop fusion | flops 32 | bytes 256 | tf_op jit(solution)/shard_map/convert_element_type | solution.py:352
  35.1 0.1 copy.17
  35.2 0.7 %convert_element_type.18.rows = s32[32]{0:T(128)} reshape(s32[4,8,1]{1,0,2:T(4,128)S(1)} %bitcast.11) | data formatting | bytes 256 | tf_op jit(solution)/shard_map/convert_element_type | solution.py:352
  35.9 2.2 %place.1 = bf16[18,64,128]{2,1,0:T(8,128)(2,1)} custom-call(s32[32]{0:T(128)} %convert_element_type.18.rows, bf16[32,64,128]{2,1,0:T(8,128)(2,1)} %bitcast.8), custom_call_target="tpu_custom_call" | custom-call | tf_op jit(solution)/shard_map/place/pallas_call | solution.py:346
  (2 shorter events, 0.0 us)
Async XLA Ops:
  0.6 33.2 %copy-start = (s32[6]{0:T(128)S(1)}, s32[6]{0:T(128)}, u32[]{:S(2)}) copy-start(s32[6]{0:T(128)} %frames.1) | copy-start | bytes 76
  0.6 32.2 %copy-start.2 = (s32[6]{0:T(128)S(1)}, s32[6]{0:T(128)}, u32[]{:S(2)}) copy-start(s32[6]{0:T(128)} %groups.1) | copy-start | bytes 76
  0.7 33.2 %copy-start.1 = (f32[6]{0:T(128)S(1)}, f32[6]{0:T(128)}, u32[]{:S(2)}) copy-start(f32[6]{0:T(128)} %rewards.1) | copy-start | bytes 76

commit v2 on v1

v2 whole, which is shorter than its diff:
```python
import functools

import jax
import jax.numpy as jnp
from jax import lax
from jax.experimental import pallas as pl
from jax.experimental.pallas import tpu as pltpu
from jax.sharding import PartitionSpec as P

MAXB = 5
GSIZE = 12
F32 = jnp.float32
BF16 = jnp.bfloat16


def main_kernel(
    dims, frames, owners, offsets, groups, rewards, embed, gain, head, latent, noise, mid,
    out, fin,
    lat, noi, mids, tokens, wown, wbuf, wt, half, vel, pred, blocks, err, ebuf,
    slot_v, slot_s, ints, intr, flts, fltr, pos_v, pos_s,
    wsend, wrecv, isend, irecv, psend, precv, gsend, grecv, esend, erecv, local_sem, load_sem,
):
    devices, mp, jm, bpc = dims
    cap = jm * mp
    c, width = embed.shape
    bt = latent.shape[2]
    nslot = owners.shape[0]
    spd = frames.shape[0]
    nchunk = tokens.shape[0]
    nblk = devices * jm
    steps, kc, _ = mids.shape
    short = nchunk <= 4
    loads = [pltpu.make_async_copy(latent, lat, load_sem.at[0])]
    for i in range(steps):
        loads.append(
            pltpu.make_async_copy(mid.at[pl.ds(i * kc, kc)], mids.at[i], load_sem.at[1 + i])
        )
    loads.append(pltpu.make_async_copy(noise, noi, load_sem.at[1 + steps]))
    for cp in loads:
        cp.start()
    me = lax.axis_index("dp")
    m = lax.axis_index("mp")
    partner = m + 1 - 2 * (m % 2)
    across = (m + 2) % 4
    diag = (partner + 2) % 4

    def copy(src, dst, ssem, rsem, dp, mp):
        return pltpu.make_async_remote_copy(
            src_ref=src, dst_ref=dst, send_sem=ssem, recv_sem=rsem,
            device_id=(dp, mp), device_id_type=pl.DeviceIdType.MESH,
        )

    barrier = pltpu.get_barrier_semaphore()
    for p in (partner, across, diag):
        pl.semaphore_signal(
            barrier, inc=1, device_id=(me, p), device_id_type=pl.DeviceIdType.MESH
        )
    for d in range(1, devices):
        pl.semaphore_signal(
            barrier, inc=1, device_id=((me + d) % devices, m),
            device_id_type=pl.DeviceIdType.MESH,
        )

    row = lax.broadcasted_iota(jnp.int32, slot_v.shape, 0)
    lane = lax.broadcasted_iota(jnp.int32, slot_v.shape, 1)
    slot_of = jnp.full(slot_v.shape, -1, jnp.int32)
    row_of = slot_of
    seen = jnp.zeros(slot_v.shape, jnp.int32)
    live = jnp.ones((1, 128), jnp.int32)
    lane1 = lax.broadcasted_iota(jnp.int32, (1, 128), 1)
    for i in range(nslot):
        if i % MAXB == 0:
            blocks_here = lax.shift_right_arithmetic(frames[i // MAXB] - 1, 5) + 1
            live = jnp.where(lane1 == i // MAXB, blocks_here, live)
        hit = lane == jnp.where(i % MAXB < blocks_here, owners[i], -1)
        new = hit & (seen == row)
        slot_of = jnp.where(new, i, slot_of)
        row_of = jnp.where(new, offsets[i], row_of)
        seen = jnp.where(hit, seen + 1, seen)
    slot_v[...] = slot_of
    ints[...] = row_of
    frow = lax.broadcasted_iota(jnp.int32, (8, 128), 0)
    flane = lax.broadcasted_iota(jnp.int32, (8, 128), 1)
    table = jnp.full((8, 128), -1.0, F32)
    for i in range(spd):
        table = jnp.where((frow == 0) & (flane == i), rewards[i], table)
        table = jnp.where((frow == 1) & (flane == i), groups[i].astype(F32), table)
    flts[...] = table
    to_smem = pltpu.make_async_copy(slot_v, slot_s, local_sem.at[0])
    to_smem.start()
    w = embed[...]
    gram = lax.dot_general(w, w, (((1,), (1,)), ((), ())), preferred_element_type=F32)
    pl.semaphore_wait(barrier, 3 + devices - 1)

    def trio(src, part):
        return [
            copy(src, wbuf.at[0, part], wsend.at[0, part], wrecv.at[0, part], me, partner),
            copy(src, wbuf.at[1, part], wsend.at[1, part], wrecv.at[1, part], me, across),
            copy(
                wbuf.at[1, part], wbuf.at[2, part], wsend.at[2, part], wrecv.at[2, part],
                me, partner,
            ),
        ]

    hc = trio(head, 1)
    wc = trio(wown, 0)
    hc[1].start()
    hc[0].start()
    ic = []
    for d in range(1, devices):
        peer = (me + d) % devices
        ic.append(copy(ints, intr.at[me], isend.at[0, d], irecv.at[0, d], peer, m))
        ic.append(copy(flts, fltr.at[me], isend.at[1, d], irecv.at[1, d], peer, m))
    for cp in ic:
        cp.start()
    intr[me] = row_of
    fltr[me] = table

    to_smem.wait()
    loads[0].wait()

    def prepare(k, z):
        for b in range(bpc):
            q = k * bpc + b
            s = jnp.maximum(slot_s[m * jm + q % jm, q // jm], 0)
            tokens[k, :, b * bt : (b + 1) * bt] = lat[s]
        x = tokens[k].astype(F32)
        y = jnp.dot(gram, x, preferred_element_type=F32, precision=lax.Precision.HIGHEST)
        ms = jnp.maximum(jnp.sum(x * y, axis=0, keepdims=True), 0.0) / width
        half[k] = 0.5 * lax.rsqrt(ms + 0.25)
        return z

    lax.fori_loop(0, nchunk, prepare, 0, unroll=short)

    folded = None
    for i in range(steps):
        wg = embed[:, i * kc : (i + 1) * kc].astype(F32) * gain[:, i * kc : (i + 1) * kc]
        hi = wg.astype(BF16)
        lo = (wg - hi.astype(F32)).astype(BF16)
        loads[1 + i].wait()
        both = jnp.dot(
            jnp.concatenate([hi, lo], axis=0), mids[i], preferred_element_type=F32
        )
        folded = both if i == 0 else folded + both
    folded = folded[:c] + folded[c:]
    wown[...] = folded.astype(BF16)
    wt[...] = folded.T.astype(BF16)
    wc[1].start()
    wc[0].start()
    hc[1].wait_recv()
    hc[2].start()

    def part(href, k):
        u = jnp.dot(wt[...], tokens[k], preferred_element_type=F32)
        h = u * half[k]
        act = (h + h * jnp.tanh(h)).astype(BF16)
        return jnp.dot(href[...], act, preferred_element_type=F32)

    def share(href, first):
        def body(k, z):
            v = part(href, k)
            vel[k] = v if first else vel[k] + v
            return z

        lax.fori_loop(0, nchunk, body, 0, unroll=short)

    share(head, True)
    hc[0].wait_recv()
    wc[0].wait_recv()
    wt[...] = wbuf[0, 0].astype(F32).T.astype(BF16)
    share(wbuf.at[0, 1], False)
    wc[1].wait_recv()
    wc[2].start()
    wt[...] = wbuf[1, 0].astype(F32).T.astype(BF16)
    share(wbuf.at[1, 1], False)
    hc[2].wait_recv()
    wc[2].wait_recv()
    wt[...] = wbuf[2, 0].astype(F32).T.astype(BF16)
    err[...] = jnp.zeros_like(err)
    erow = lax.broadcasted_iota(jnp.int32, err.shape, 0)
    loads[1 + steps].wait()

    def sending(q):
        o, jj = q // jm, q % jm
        return copy(
            pred.at[q], blocks.at[(m * devices + me) * jm + jj],
            psend.at[q], precv.at[me * jm + jj], o, m,
        )

    def keeping(q):
        return pltpu.make_async_copy(
            pred.at[q], blocks.at[(m * devices + me) * jm + q % jm], psend.at[q]
        )

    def last(step, z):
        k = (me * jm // bpc + 1 + step) % nchunk
        v = vel[k] + part(wbuf.at[2, 1], k)
        for b in range(bpc):
            q = k * bpc + b
            vb = v[:, b * bt : (b + 1) * bt]
            pred[q] = vb.astype(BF16)

            @pl.when(q // jm != me)
            def _():
                sending(q).start()

            @pl.when(q // jm == me)
            def _():
                keeping(q).start()

            s = slot_s[m * jm + q % jm, q // jm]
            e = noi[jnp.maximum(s, 0)].astype(F32) + vb
            e = jnp.sum(e * e, axis=0, keepdims=True)
            sample = jnp.where(s < 0, -1, s // MAXB)
            err[...] += jnp.where(erow == sample, e, 0.0)
        return z

    lax.fori_loop(0, nchunk, last, 0, unroll=short)
    ec = []
    for i, p in enumerate((partner, across, diag)):
        cp = copy(err, ebuf.at[i], esend.at[i], erecv.at[i], me, p)
        cp.start()
        ec.append(cp)

    def moves(n, src, jj):
        at = blocks.at[(m * devices + src) * jm + jj]
        far = blocks.at[(across * devices + src) * jm + jj]
        return (
            copy(at, at, gsend.at[0, n], grecv.at[0, n], me, across),
            copy(at, at, gsend.at[1, n], grecv.at[1, n], me, partner),
            copy(far, far, gsend.at[2, n], grecv.at[2, n], me, partner),
        )

    gc = []
    for d in range(devices):
        src = (me - d + devices) % devices
        for jj in range(jm):
            trip = moves(d * jm + jj, src, jj)
            gc.append(trip)
            if d == 0:
                keeping(me * jm + jj).wait()
            else:
                pltpu.make_async_remote_copy(
                    src_ref=pred.at[0], dst_ref=blocks.at[(m * devices + src) * jm + jj],
                    send_sem=psend.at[0], recv_sem=precv.at[src * jm + jj],
                    device_id=(src, m), device_id_type=pl.DeviceIdType.MESH,
                ).wait_recv()
            trip[0].start()
            trip[1].start()
        if d == 0:
            for cp in ic:
                cp.wait_recv()
            code = jnp.full(slot_v.shape, -1, jnp.int32)
            for j in range(cap):
                code = jnp.where(row == j, (j // jm * devices) * jm + j % jm, code)
            pos = jnp.zeros(slot_v.shape, jnp.int32)
            mean = jnp.zeros((1, 128), F32)
            square = jnp.zeros((1, 128), F32)
            for s in range(devices):
                want = jnp.max(
                    jnp.where((lane == me) & (row < cap), intr[s], -1), axis=1, keepdims=True
                )
                pos = jnp.maximum(pos, jnp.where(want == lane, code + s * jm, 0))
            pos_v[...] = jnp.broadcast_to(jnp.max(pos, axis=0, keepdims=True), pos_v.shape)
            place = pltpu.make_async_copy(pos_v, pos_s, local_sem.at[1])
            place.start()
            every = fltr[:, 0, :]
            group = fltr[:, 1, :]
            for i in range(spd):
                mine = jnp.where(group == groups[i].astype(F32), every, 0.0)
                one = jnp.sum(jnp.sum(mine, axis=0, keepdims=True), axis=1, keepdims=True)
                two = jnp.sum(
                    jnp.sum(mine * mine, axis=0, keepdims=True), axis=1, keepdims=True
                )
                mean = jnp.where(lane1 == i, one / GSIZE, mean)
                square = jnp.where(lane1 == i, two / GSIZE, square)
            own = table[0:1]
            gained = (own - mean) * lax.rsqrt(square - mean * mean + 0.25)
    for trip in gc:
        trip[0].wait_recv()
        trip[2].start()
    for i in range(3):
        ec[i].wait_recv()
    total = jnp.sum(err[...] + ebuf[0] + ebuf[1] + ebuf[2], axis=1, keepdims=True)
    elane = lax.broadcasted_iota(jnp.int32, err.shape, 1)
    total = jnp.sum(jnp.where(erow == elane, total, 0.0), axis=0, keepdims=True)
    logp = -0.5 * total / (live * bt * c).astype(F32)
    fin[...] = jnp.where(frow == 0, logp, gained)
    place.wait()
    for trip in gc:
        trip[1].wait_recv()
        trip[2].wait_recv()

    for r in range(out.shape[0]):
        out[r] = blocks[pos_s[0, r]]
    for cp in ic:
        cp.wait_send()
    for q in range(nblk):

        @pl.when(q // jm != me)
        def _():
            sending(q).wait_send()

    for trip in gc:
        for cp in trip:
            cp.wait_send()
    for i in range(3):
        hc[i].wait_send()
        wc[i].wait_send()
        ec[i].wait_send()


def local(
    frames, owners, offsets, groups, latent, noise_blocks, rewards,
    embed_weight, norm_gain, mid_weight, head_weight,
):
    spd = frames.shape[0]
    devices = lax.axis_size("dp")
    mp = lax.axis_size("mp")
    nslot, c, bt = latent.shape
    width = embed_weight.shape[1]
    hidden = mid_weight.shape[1]
    pair_cap = (nslot + devices - 1) // devices
    jm = (pair_cap + mp - 1) // mp
    cap = jm * mp
    bpc = 2 if devices * jm % 2 == 0 else 1
    nchunk = devices * jm // bpc
    dims = (devices, mp, jm, bpc)
    rows8 = (spd + 7) // 8 * 8
    cap8 = (cap + 7) // 8 * 8
    steps = 4
    kc = width // steps
    smem = pl.BlockSpec(memory_space=pltpu.SMEM)
    vmem = pl.BlockSpec(memory_space=pltpu.VMEM)
    hbm = pl.BlockSpec(memory_space=pl.ANY)
    shape = jax.ShapeDtypeStruct
    dma = pltpu.SemaphoreType.DMA
    nblk = devices * jm
    prediction, fin = pl.pallas_call(
        functools.partial(main_kernel, dims),
        in_specs=[smem] * 5 + [vmem] * 3 + [hbm] * 3,
        out_specs=[vmem] * 2,
        out_shape=[shape((3 * spd, c, bt), BF16), shape((8, 128), F32)],
        scratch_shapes=[
            pltpu.VMEM((nslot, c, bt), BF16),
            pltpu.VMEM((nslot, c, bt), BF16),
            pltpu.VMEM((steps, kc, hidden), BF16),
            pltpu.VMEM((nchunk, c, bpc * bt), BF16),
            pltpu.VMEM((c, hidden), BF16),
            pltpu.VMEM((3, 2, c, hidden), BF16),
            pltpu.VMEM((hidden, c), BF16),
            pltpu.VMEM((nchunk, 1, bpc * bt), F32),
            pltpu.VMEM((nchunk, c, bpc * bt), F32),
            pltpu.VMEM((nblk, c, bt), BF16),
            pltpu.VMEM((mp * nblk, c, bt), BF16),
            pltpu.VMEM((rows8, bt), F32),
            pltpu.VMEM((3, rows8, bt), F32),
            pltpu.VMEM((cap8, 128), jnp.int32),
            pltpu.SMEM((cap8, 128), jnp.int32),
            pltpu.VMEM((cap8, 128), jnp.int32),
            pltpu.VMEM((devices, cap8, 128), jnp.int32),
            pltpu.VMEM((8, 128), F32),
            pltpu.VMEM((devices, 8, 128), F32),
            pltpu.VMEM((8, 128), jnp.int32),
            pltpu.SMEM((8, 128), jnp.int32),
            dma((3, 2)), dma((3, 2)),
            dma((2, devices)), dma((2, devices)),
            dma((nblk,)), dma((nblk,)),
            dma((3, nblk)), dma((3, nblk)),
            dma((3,)), dma((3,)),
            dma((2,)), dma((steps + 2,)),
        ],
        compiler_params=pltpu.CompilerParams(collective_id=0, has_side_effects=True),
        name="regroup",
    )(
        frames, owners, offsets, groups, rewards,
        embed_weight, norm_gain.reshape(1, width), head_weight.T,
        latent, noise_blocks, mid_weight,
    )
    return (prediction, fin[0, :spd], fin[1, :spd])


def solution(mesh):
    placed = (
        P("dp"),
        P("dp"),
        P("dp"),
        P("dp"),
        P("dp", None, None),
        P("dp", None, None),
        P("dp"),
        P(),
        P(),
        P(None, "mp"),
        P("mp", None),
    )
    return jax.shard_map(
        local,
        mesh=mesh,
        in_specs=placed,
        out_specs=(P("dp", None, None), P("dp"), P("dp")),
        check_vma=False,
    )
```

time: 38.4 us -> 30.3 us (0.79)
  Pallas kernels: 33.3 us -> 26.4 us
  other arithmetic: 2.29 us -> 0 us
  local copies, waits for them, and re-layouts: 1.79 us -> 2.97 us
    pallas_call x3 -> x1, Pallas kernels: 33.3 us -> 26.4 us  [local(): pl.pallas_call(functools.partial(main_kernel, dims), in_specs=[smem] * 5...]
    unnamed x6 -> x1, local copies, waits for them, and re-layouts: 0.01 us -> 1.69 us
    squeeze x0 -> x1, local copies, waits for them, and re-layouts: none -> 1.27 us  [local(): return (prediction, fin[0, :spd], fin[1, :spd])]
    reduce_sum x2 -> x0, other arithmetic: 0.98 us -> none  [the longest x1 0.8 us: local(): jnp.sum(errs[:spd], axis=1)]
    slice x1 -> x0, local copies, waits for them, and re-layouts: 0.86 us -> none  [local(): same = groups.astype(F32)[:, None] == infos[:, 2, :spd].reshape(-1)[None, :]]
    convert_element_type x2 -> x0, other arithmetic: 0.76 us -> none  [the longest x1 0.76 us: local(): where.astype(jnp.int32)]
    convert_element_type x2 -> x0, local copies, waits for them, and re-layouts: 0.76 us -> none  [local(): where.astype(jnp.int32)]
    div x1 -> x0, other arithmetic: 0.53 us -> none  [local(): advantage = (rewards - mean) / jnp.sqrt(meansq - mean * mean + 0.25)]
where the time goes in v2:
time: 30.3 us; the launch traced here: 30 us
  Pallas kernels  26.4 us (87%)
  local copies, waits for them, and re-layouts  2.97 us (10%)
  between operations  0.64 us (2%)
    pallas_call x1, Pallas kernels, local(): pl.pallas_call(functools.partial(main_kernel, dims), in_specs=[smem] * 5...  26.4 us
    unnamed x1, local copies, waits for them, and re-layouts  1.69 us
    squeeze x1, local copies, waits for them, and re-layouts, local(): return (prediction, fin[0, :spd], fin[1, :spd])  1.27 us

profile of v2, /device:TPU:0, one launch (start us, length us, event | category | flops | bytes accessed | tf_op | source)
XLA Modules:
  0.0 30.0 jit_solution(279121516660783526)
XLA Ops:
  0.6 26.4 %regroup.1 = (bf16[18,64,128]{2,1,0:T(8,128)(2,1)}, f32[8,128]{1,0:T(8,128)}) custom-call(s32[6]{0:T(128)} %frames.1, s32[30]{0:T(128)} %owners.1, s32[30]{0:T(128)} %offsets.1, s32[6]{0:T(128)} %groups.1, f32[6]{0:T(128)} %rewards.1, bf16[64,3072]{1,0:T(8,128)(2,1)} %embed.1, f32[1,3072]{1,0:T(1,128)} %bitcast.7, bf16[64,768]{1,0:T(8,128)(2,1)} %bitcast.6, ...), custom_call_target="tpu_custom_call" | custom-call | tf_op jit(solution)/shard_map/regroup/pallas_call | solution.py:339
  27.1 1.3 %slice_bitcast_fusion = (f32[6]{0:T(128)}, f32[6]{0:T(128)}) fusion(f32[8,128]{1,0:T(8,128)} %get-tuple-element.6), kind=kLoop, calls=%fused_computation | loop fusion | bytes 96 | tf_op jit(solution)/shard_map/squeeze | solution.py:380
  28.3 1.7 %copy.15 = bf16[18,64,128]{2,1,0:T(8,128)(2,1)} copy(bf16[18,64,128]{2,1,0:T(8,128)(2,1)} %get-tuple-element.12) | data formatting | bytes 589824

commit v3 on v2

--- a/solution.py
+++ b/solution.py
@@ -310,6 +310,13 @@
         ec[i].wait_send()
 
 
+def finish_kernel(fin, rows, out, logp, gained):
+    out[...] = rows[...]
+    for i in range(logp.shape[0]):
+        logp[i] = fin[0, i]
+        gained[i] = fin[1, i]
+
+
 def local(
     frames, owners, offsets, groups, latent, noise_blocks, rewards,
     embed_weight, norm_gain, mid_weight, head_weight,
@@ -323,7 +330,7 @@
     pair_cap = (nslot + devices - 1) // devices
     jm = (pair_cap + mp - 1) // mp
     cap = jm * mp
-    bpc = 2 if devices * jm % 2 == 0 else 1
+    bpc = 4 if devices * jm % 4 == 0 else 1
     nchunk = devices * jm // bpc
     dims = (devices, mp, jm, bpc)
     rows8 = (spd + 7) // 8 * 8
@@ -336,7 +343,7 @@
     shape = jax.ShapeDtypeStruct
     dma = pltpu.SemaphoreType.DMA
     nblk = devices * jm
-    prediction, fin = pl.pallas_call(
+    placed_rows, fin = pl.pallas_call(
         functools.partial(main_kernel, dims),
         in_specs=[smem] * 5 + [vmem] * 3 + [hbm] * 3,
         out_specs=[vmem] * 2,
@@ -377,7 +384,13 @@
         embed_weight, norm_gain.reshape(1, width), head_weight.T,
         latent, noise_blocks, mid_weight,
     )
-    return (prediction, fin[0, :spd], fin[1, :spd])
+    return pl.pallas_call(
+        finish_kernel,
+        in_specs=[smem, vmem],
+        out_specs=[vmem, smem, smem],
+        out_shape=[shape((3 * spd, c, bt), BF16), shape((spd,), F32), shape((spd,), F32)],
+        name="finish",
+    )(fin, placed_rows)
 
 
 def solution(mesh):

time: 30.3 us -> 27.5 us (0.908)
  local copies, waits for them, and re-layouts: 2.97 us -> 0 us
    pallas_call x0 -> x1, Pallas kernels: none -> 1.72 us  [local(): pl.pallas_call(finish_kernel, in_specs=[smem, vmem], out_specs=[vmem, sme...]
    unnamed x1 -> x0, local copies, waits for them, and re-layouts: 1.69 us -> none
    pallas_call x1, Pallas kernels: 26.4 us -> 25 us  [local(): pl.pallas_call(functools.partial(main_kernel, dims), in_specs=[smem] * 5...]
    squeeze x1 -> x0, local copies, waits for them, and re-layouts: 1.27 us -> none  [local(): return (prediction, fin[0, :spd], fin[1, :spd])]
where the time goes in v3:
time: 27.5 us; the launch traced here: 27.3 us
  Pallas kernels  26.7 us (97%)
  between operations  0.64 us (2%)
    pallas_call x1, Pallas kernels, local(): pl.pallas_call(functools.partial(main_kernel, dims), in_specs=[smem] * 5...  25 us
    pallas_call x1, Pallas kernels, local(): pl.pallas_call(finish_kernel, in_specs=[smem, vmem], out_specs=[vmem, sme...  1.72 us

profile of v3, /device:TPU:0, one launch (start us, length us, event | category | flops | bytes accessed | tf_op | source)
XLA Modules:
  0.0 27.3 jit_solution(735739438211518686)
XLA Ops:
  0.6 25.0 %regroup.1 = (bf16[18,64,128]{2,1,0:T(8,128)(2,1)}, f32[8,128]{1,0:T(8,128)}) custom-call(s32[6]{0:T(128)} %frames.1, s32[30]{0:T(128)} %owners.1, s32[30]{0:T(128)} %offsets.1, s32[6]{0:T(128)} %groups.1, f32[6]{0:T(128)} %rewards.1, bf16[64,3072]{1,0:T(8,128)(2,1)} %embed.1, f32[1,3072]{1,0:T(1,128)} %bitcast.3, bf16[64,768]{1,0:T(8,128)(2,1)} %bitcast.2, ...), custom_call_target="tpu_custom_call" | custom-call | tf_op jit(solution)/shard_map/regroup/pallas_call | solution.py:346
  25.6 1.7 %finish.1 = (bf16[18,64,128]{2,1,0:T(8,128)(2,1)}, f32[6]{0:T(128)}, f32[6]{0:T(128)}) custom-call(f32[8,128]{1,0:T(8,128)} %get-tuple-element.5.fin, bf16[18,64,128]{2,1,0:T(8,128)(2,1)} %get-tuple-element.6.rows), custom_call_target="tpu_custom_call" | custom-call | tf_op jit(solution)/shard_map/finish/pallas_call | solution.py:387
